TPU v7x, 256 devices: a whole 4x4x8 slice. The times are simulated.
256 devices in a mesh: lev: 8 (over z), wav: 32 (over y, x, core).
Axes of the slice: x: 4, y: 4, z: 8, core: 2. Of those that a mesh axis runs over, the one named last changes fastest.
Arguments:
- grid_field: float32 [16, 1216, 1216], P('lev', 'wav'), may hold values from -6 to 6
- truncation_limit: int32 [1216], replicated, may hold values from -1 to 607, as said below
- diffusion_order: int32 [16], P('lev'), may hold values from 1 to 4
- diffusion_strength: float32 [16], P('lev'), may hold values from 2 to 50
- mass_weight: float32 [16], P('lev'), may hold values from 0.25 to 4
Outputs:
- filtered: float32 [16, 1216, 1216], P('lev', 'wav')
- energies: float32 [16], P('lev')
- total_energy: float32 [], replicated
Inputs may be any that keep to these rules, and one draw needn't show every extreme that they name: `truncation_limit`: the largest |wavenumber(q)| kept at index p, with wavenumber(m) = m below 608 and m - 1216 otherwise; the kept set is an ellipse about wavenumber zero; the value at p equals the value at 1216 - p; -1 where nothing is kept; the value at p = 0 is 607.
All inputs are finite; a program needn't handle non-finite values.
Results may differ from a plain program's by a relative error of at most 0.000071.
Values sent between devices are 32-bit elements.
A program may use at most 64 MiB of HBM per device.

v0:
```python
import math

import jax
import jax.numpy as jnp
import numpy as np
from jax import lax
from jax.experimental import pallas as pl
from jax.experimental.pallas import tpu as pltpu
from jax.sharding import PartitionSpec as P

MESH = pl.DeviceIdType.MESH
f32, bf16 = jnp.float32, jnp.bfloat16

LENGTH = 1216
HALF = LENGTH // 2
PAD = 640
ROWS = 38
PITCH = 40
GROUP = 76
PEERS = 32


def basis(parity):
    index = np.arange(HALF, dtype=np.int64)
    if parity == 0:
        phase = (index[:, None] * index[None, :]) % HALF
        angle = phase.astype(np.float64) * (2.0 * math.pi / HALF)
    else:
        phase = ((2 * index[:, None] + 1) * (2 * index[None, :] + 1)) % (4 * HALF)
        angle = phase.astype(np.float64) * (2.0 * math.pi / (4 * HALF))
    table = np.zeros((HALF, PAD), np.float32)
    table[:, :HALF] = np.cos(angle) + np.sin(angle)
    high = table.astype(bf16)
    low = (table - high.astype(np.float32)).astype(bf16)
    return high, low


def dot(a, b):
    return jnp.dot(a, b, preferred_element_type=f32)


def split(values):
    high = values.astype(bf16)
    return high, (values - high.astype(f32)).astype(bf16)


def lanes(shape):
    return lax.broadcasted_iota(jnp.int32, shape, len(shape) - 1)


def pack(block):
    third, fourth = block[24:32], block[32:40]
    lane = lanes((8, 128))
    tail = [
        pltpu.roll(third, 76, 1),
        pltpu.roll(fourth, 76, 1),
        jnp.where(lane < 100, pltpu.roll(third, 24, 1), pltpu.roll(fourth, 48, 1)),
    ]
    return [jnp.where(lane < GROUP, block[8 * i : 8 * i + 8], tail[i]) for i in range(3)]


def unpack(first, second, third):
    lane = lanes((8, 128))
    return [
        first,
        second,
        third,
        jnp.where(lane < 52, pltpu.roll(first, 52, 1), pltpu.roll(third, 104, 1)),
        jnp.where(lane < 52, pltpu.roll(second, 52, 1), pltpu.roll(third, 80, 1)),
    ]


def chip_of(parity, group):
    return (group // 2) * 4 + (group % 2) * 2 + parity


def kernel(
    x_ref, limit_ref, order_ref, strength_ref, mass_ref, eh_hbm, el_hbm, oh_hbm, ol_hbm,
    out_ref, energy_ref, total_ref,
    tables, xs, ybuf, wbuf, gbuf, damp,
    send1, recv1, send2, recv2, esend, erecv, lsend, lrecv,
    table_sem, s1, r1, s2, r2, es, er, ls, lr,
):
    lev = lax.axis_index("lev")
    me = lax.axis_index("wav")
    core = me % 2
    chip_x = (me // 2) % 4
    parity_me = chip_x % 2
    group_me = (me // 8) * 2 + chip_x // 2

    loads = [
        pltpu.make_async_copy(source, tables.at[i, pl.ds(0, HALF)], table_sem.at[i])
        for i, source in enumerate((eh_hbm, el_hbm, oh_hbm, ol_hbm))
    ]
    for load in loads:
        load.start()

    barrier = pltpu.get_barrier_semaphore()

    def greet(k, carry):
        pl.semaphore_signal(barrier, inc=1, device_id=(lev, (me + k) % PEERS), device_id_type=MESH)
        return carry

    def greet_lev(k, carry):
        pl.semaphore_signal(barrier, inc=1, device_id=((lev + k) % 8, me), device_id_type=MESH)
        return carry

    lax.fori_loop(1, PEERS, greet, 0)
    lax.fori_loop(1, 8, greet_lev, 0)

    tables[:, HALF:, :] = jnp.zeros((4, PAD - HALF, PAD), bf16)
    xs[:, 32:40, :] = jnp.zeros((2, 8, 1280), f32)
    xs[:, :, 1152:] = jnp.zeros((2, 40, 128), f32)
    for s in range(2):
        xs[s, :ROWS, :LENGTH] = x_ref[s]
    lane640 = lanes((PITCH, PAD))
    folded = [[], []]
    for s in range(2):
        whole = xs[s]
        lower = jnp.where(lane640 < HALF, whole[:, :PAD], 0.0)
        upper = pltpu.roll(whole, 1280 - HALF, 1)[:, :PAD]
        folded[0].append(lower + upper)
        folded[1].append(lower - upper)

    def spread(parity):
        for g in range(8):
            tile, offset = divmod(GROUP * g, 128)
            lane = lanes((80, 128))
            piece = ybuf[:, 128 * tile : 128 * tile + 128]
            if offset:
                piece = pltpu.roll(piece, 128 - offset, 1)
            if offset + GROUP > 128:
                after = pltpu.roll(ybuf[:, 128 * tile + 128 : 128 * tile + 256], 128 - offset, 1)
                piece = jnp.where(lane < 128 - offset, piece, after)
            for c in range(2):
                packed = pack(piece[PITCH * c : PITCH * c + PITCH])
                e = chip_of(parity, g) * 2 + c
                for i in range(3):
                    send1[e, 8 * i : 8 * i + 8, :] = packed[i]

    def exchange(send, recv, ssem, rsem, e):
        return pltpu.make_async_remote_copy(
            src_ref=send.at[e], dst_ref=recv.at[me], send_sem=ssem.at[e], recv_sem=rsem.at[me],
            device_id=(lev, e), device_id_type=MESH,
        )

    def await_from(send, recv, ssem, rsem, e):
        pltpu.make_async_remote_copy(
            src_ref=send.at[e], dst_ref=recv.at[e], send_sem=ssem.at[e], recv_sem=rsem.at[e],
            device_id=(lev, e), device_id_type=MESH,
        ).wait_recv()

    def await_sent(send, recv, ssem, rsem, e):
        exchange(send, recv, ssem, rsem, e).wait_send()

    first_copy = (send1, recv1, s1, r1)
    second_copy = (send2, recv2, s2, r2)
    energy_copy = (esend, erecv, es, er)

    def over_peers(body):
        def step(k, carry):
            body((me + k) % PEERS)
            return carry

        lax.fori_loop(1, PEERS, step, 0)

    for parity in range(2):
        high, low = split(jnp.concatenate(folded[parity], axis=0))
        loads[2 * parity].wait()
        loads[2 * parity + 1].wait()
        both = dot(jnp.concatenate([high, low], axis=0), tables[2 * parity])
        ybuf[...] = both[:80] + both[80:] + dot(high, tables[2 * parity + 1])
        spread(parity)
    pl.semaphore_wait(barrier, PEERS - 1 + 7)
    over_peers(lambda e: exchange(*first_copy, e).start())
    recv1[me] = send1[me]

    order = order_ref[core]
    strength = strength_ref[core]

    def place(l, carry):
        value = limit_ref[2 * (GROUP * group_me + l) + parity_me]
        return jnp.where(lanes((8, 128)) == l, value, carry)

    limits = lax.fori_loop(0, GROUP, place, jnp.full((8, 128), -1, jnp.int32))[:1]
    lane1 = lanes((1, 128))
    index1 = GROUP * group_me + lane1
    twice1 = 2 * index1 + parity_me
    wave1 = jnp.minimum(twice1, LENGTH - twice1).astype(f32)
    index2 = lax.broadcasted_iota(jnp.int32, (PAD, 128), 0)
    for parity in range(2):
        twice2 = 2 * index2 + parity
        wave2 = jnp.minimum(twice2, LENGTH - twice2)
        first = wave2.astype(f32)
        radius = (wave1 * wave1 + first * first) / float(HALF) ** 2
        square = radius * radius
        powered = jnp.where(order >= 2, square, radius)
        powered = jnp.where(order >= 3, square * radius, powered)
        powered = jnp.where(order >= 4, square * square, powered)
        kept = (wave2 <= limits) & (lane1 < GROUP) & (index2 < HALF)
        damp[parity] = jnp.where(
            kept, (1.0 / float(LENGTH) ** 2) / (1.0 + strength * powered), 0.0
        )

    wbuf[:, HALF:, :] = jnp.zeros((2, PAD - HALF, 128), f32)
    over_peers(lambda e: await_from(*first_copy, e))
    for d in range(16):
        sums = [recv1[d, 8 * i : 8 * i + 8] + recv1[d + 16, 8 * i : 8 * i + 8] for i in range(3)]
        differences = [recv1[d, 8 * i : 8 * i + 8] - recv1[d + 16, 8 * i : 8 * i + 8] for i in range(3)]
        for parity, packed in enumerate((sums, differences)):
            pieces = unpack(*packed)
            for i in range(5):
                count = 8 if i < 4 else ROWS - 32
                start = ROWS * d + 8 * i
                wbuf[parity, start : start + count, :] = pieces[i][:count]
    energy = jnp.zeros((8, 128), f32)
    spectra = []
    for parity in range(2):
        high, low = split(wbuf[parity])
        both = dot(tables[2 * parity], jnp.concatenate([high, low], axis=1))
        spectrum = both[:, :128] + both[:, 128:] + dot(tables[2 * parity + 1], high)
        damped = spectrum * damp[parity]
        energy = energy + jnp.sum((damped * damped).reshape(PAD // 8, 8, 128), axis=0)
        high, low = split(damped)
        spectra.append(jnp.concatenate([high, low], axis=1))
    partial_value = jnp.full((8, 128), jnp.sum(energy))
    esend[...] = partial_value

    def energy_to(e):
        return pltpu.make_async_remote_copy(
            src_ref=esend, dst_ref=erecv.at[me], send_sem=es.at[e], recv_sem=er.at[me],
            device_id=(lev, e), device_id_type=MESH,
        )

    def energy_from(e):
        return pltpu.make_async_remote_copy(
            src_ref=esend, dst_ref=erecv.at[e], send_sem=es.at[e], recv_sem=er.at[e],
            device_id=(lev, e), device_id_type=MESH,
        )

    def level_to(e):
        return pltpu.make_async_remote_copy(
            src_ref=lsend, dst_ref=lrecv.at[lev], send_sem=ls.at[e], recv_sem=lr.at[lev],
            device_id=(e, me), device_id_type=MESH,
        )

    def level_from(e):
        return pltpu.make_async_remote_copy(
            src_ref=lsend, dst_ref=lrecv.at[e], send_sem=ls.at[e], recv_sem=lr.at[e],
            device_id=(e, me), device_id_type=MESH,
        )

    over_peers(lambda e: energy_to(e).start())
    erecv[me] = partial_value

    for part in range(2):
        rows = slice(304 * part, 304 * part + 304)
        for parity in range(2):
            both = dot(tables[2 * parity, rows], spectra[parity])
            gbuf[parity, rows] = (
                both[:, :128] + both[:, 128:]
                + dot(tables[2 * parity + 1, rows], spectra[parity][:, :128])
            )
        if part == 1:
            gbuf[:, HALF:] = jnp.zeros((2, PAD - HALF, 128), f32)
        for d in range(8 * part, 8 * part + 8):
            count = PITCH if d % 8 < 7 or part == 1 else ROWS
            even = gbuf[0, ROWS * d : ROWS * d + count]
            odd = gbuf[1, ROWS * d : ROWS * d + count]
            if count < PITCH:
                even = jnp.concatenate([even, jnp.zeros((PITCH - count, 128), f32)], axis=0)
                odd = jnp.concatenate([odd, jnp.zeros((PITCH - count, 128), f32)], axis=0)
            for e, block in ((d, even + odd), (d + 16, even - odd)):
                packed = pack(block)
                for i in range(3):
                    send2[e, 8 * i : 8 * i + 8, :] = packed[i]
    over_peers(lambda e: exchange(*second_copy, e).start())
    recv2[me] = send2[me]

    over_peers(lambda e: energy_from(e).wait_recv())
    sums = [erecv[0], erecv[1]]
    for e in range(2, PEERS):
        sums[e % 2] = sums[e % 2] + erecv[e]
    weighted = mass_ref[0] * sums[0] + mass_ref[1] * sums[1]
    lsend[...] = weighted
    energy_ref[0] = sums[0][0, 0]
    energy_ref[1] = sums[1][0, 0]

    def over_levels(body):
        def step(k, carry):
            body((lev + k) % 8)
            return carry

        lax.fori_loop(1, 8, step, 0)

    over_levels(lambda e: level_to(e).start())
    lrecv[lev] = weighted

    over_peers(lambda e: await_from(*second_copy, e))
    results = []
    for parity in range(2):
        halves = []
        for c in range(2):
            tiles = [None] * 5
            for g in range(8):
                e = chip_of(parity, g) * 2 + c
                pieces = unpack(*[recv2[e, 8 * i : 8 * i + 8] for i in range(3)])
                tile, offset = divmod(GROUP * g, 128)
                block = jnp.concatenate(pieces, axis=0)
                if offset:
                    block = pltpu.roll(block, offset, 1)
                lane = lanes((PITCH, 128))
                if tiles[tile] is None:
                    tiles[tile] = block
                else:
                    tiles[tile] = jnp.where(lane < offset, tiles[tile], block)
                if offset + GROUP > 128:
                    tiles[tile + 1] = block
            tiles[4] = jnp.where(lanes((PITCH, 128)) < HALF - 512, tiles[4], 0.0)
            halves.append(jnp.concatenate(tiles, axis=1))
        high, low = split(jnp.concatenate(halves, axis=0))
        both = dot(jnp.concatenate([high, low], axis=0), tables[2 * parity])
        results.append(both[:80] + both[80:] + dot(high, tables[2 * parity + 1]))
    sums = results[0] + results[1]
    differences = results[0] - results[1]
    blank = jnp.zeros((80, PAD), f32)
    whole = jnp.concatenate([sums, blank], axis=1) + pltpu.roll(
        jnp.concatenate([differences, blank], axis=1), HALF, 1
    )
    for s in range(2):
        out_ref[s] = whole[PITCH * s : PITCH * s + ROWS, :LENGTH]

    over_levels(lambda e: level_from(e).wait_recv())
    total = lrecv[0]
    for e in range(1, 8):
        total = total + lrecv[e]
    total_ref[0] = total[0, 0] / 16.0

    over_peers(lambda e: await_sent(*first_copy, e))
    over_peers(lambda e: energy_to(e).wait_send())
    over_peers(lambda e: await_sent(*second_copy, e))
    over_levels(lambda e: level_to(e).wait_send())


def local(grid_field, truncation_limit, diffusion_order, diffusion_strength, mass_weight):
    table_list = [jnp.asarray(t) for parity in range(2) for t in basis(parity)]
    vmem = pl.BlockSpec(memory_space=pltpu.VMEM)
    smem = pl.BlockSpec(memory_space=pltpu.SMEM)
    anywhere = pl.BlockSpec(memory_space=pl.ANY)
    dma = pltpu.SemaphoreType.DMA
    filtered, energies, total = pl.pallas_call(
        kernel,
        out_shape=(
            jax.ShapeDtypeStruct(grid_field.shape, f32),
            jax.ShapeDtypeStruct((2,), f32),
            jax.ShapeDtypeStruct((1,), f32),
        ),
        in_specs=[vmem, smem, smem, smem, smem] + [anywhere] * 4,
        out_specs=(vmem, smem, smem),
        scratch_shapes=[
            pltpu.VMEM((4, PAD, PAD), bf16),
            pltpu.VMEM((2, PITCH, 1280), f32),
            pltpu.VMEM((80, PAD), f32),
            pltpu.VMEM((2, PAD, 128), f32),
            pltpu.VMEM((2, PAD, 128), f32),
            pltpu.VMEM((2, PAD, 128), f32),
            pltpu.VMEM((PEERS, 24, 128), f32),
            pltpu.VMEM((PEERS, 24, 128), f32),
            pltpu.VMEM((PEERS, 24, 128), f32),
            pltpu.VMEM((PEERS, 24, 128), f32),
            pltpu.VMEM((8, 128), f32),
            pltpu.VMEM((PEERS, 8, 128), f32),
            pltpu.VMEM((8, 128), f32),
            pltpu.VMEM((8, 8, 128), f32),
            dma((4,)),
            dma((PEERS,)), dma((PEERS,)), dma((PEERS,)), dma((PEERS,)),
            dma((PEERS,)), dma((PEERS,)), dma((8,)), dma((8,)),
        ],
        compiler_params=pltpu.CompilerParams(
            collective_id=0, has_side_effects=True, vmem_limit_bytes=48 * 1024 * 1024
        ),
    )(grid_field, truncation_limit, diffusion_order, diffusion_strength, mass_weight, *table_list)
    return filtered, energies, total.reshape(())


def solution(mesh):
    placed = (P("lev", "wav", None), P(), P("lev"), P("lev"), P("lev"))
    return jax.shard_map(
        local,
        mesh=mesh,
        in_specs=placed,
        out_specs=(P("lev", "wav", None), P("lev"), P()),
        check_vma=False,
    )
```

profile of v0, /device:TPU:1, one launch (start us, length us, event | category | flops | bytes accessed | tf_op | source)
XLA Modules:
  0.0 43.6 jit_solution(15969615099012869805)
XLA Ops:
  0.6 0.0 copy-start
  0.6 0.0 copy-start.7
  0.7 0.0 copy-start.6
  0.7 0.0 copy-start.5
  0.7 0.0 copy-start.4
  0.7 1.1 %copy.12.x_ref = f32[2,38,1216]{2,1,0:T(8,128)S(1)} copy(f32[2,38,1216]{2,0,1:T(2,128)} %param.9) | data formatting | bytes 739328 | tf_op args[0]
  1.8 0.1 copy-done
  1.9 0.0 copy-done.7
  1.9 0.0 copy-done.6
  1.9 0.0 copy-done.5
  1.9 0.0 copy-done.4
  1.9 0.0 copy-start.1
  1.9 1.1 %copy-done.1 = bf16[608,640]{1,0:T(8,128)(2,1)S(1)} copy-done((bf16[608,640]{1,0:T(8,128)(2,1)S(1)}, bf16[608,640]{1,0:T(8,128)(2,1)}, u32[]{:S(2)}) %copy-start.1) | copy-done | bytes 778264
  3.0 0.0 copy-start.2
  3.0 1.1 %copy-done.2 = bf16[608,640]{1,0:T(8,128)(2,1)S(1)} copy-done((bf16[608,640]{1,0:T(8,128)(2,1)S(1)}, bf16[608,640]{1,0:T(8,128)(2,1)}, u32[]{:S(2)}) %copy-start.2) | copy-done | bytes 778264
  4.2 0.0 copy-start.3
  4.2 1.1 %copy-done.3 = bf16[608,640]{1,0:T(8,128)(2,1)S(1)} copy-done((bf16[608,640]{1,0:T(8,128)(2,1)S(1)}, bf16[608,640]{1,0:T(8,128)(2,1)}, u32[]{:S(2)}) %copy-start.3) | copy-done | bytes 778264
  5.3 35.0 %shard_map.112 = (f32[2,38,1216]{2,1,0:T(8,128)S(1)}, f32[2]{0:T(128)S(1)}, f32[1]{0:T(128)}) custom-call(f32[2,38,1216]{2,1,0:T(8,128)S(1)} %copy.12.x_ref, s32[1216]{0:T(1024)S(1)} %copy-done.4, s32[2]{0:T(128)S(1)} %copy-done.5, f32[2]{0:T(128)S(1)} %copy-done.6, f32[2]{0:T(128)S(1)} %copy-done.7, bf16[608,640]{1,0:T(8,128)(2,1)S(1)} %copy-done.3, ...), custom_call_target="tpu_custom_call" | custom-call | tf_op jit(solution)/shard_map/pallas_call | solution.py:351
  40.3 0.9 %copy.13 = f32[2,38,1216]{2,0,1:T(2,128)} copy(f32[2,38,1216]{2,1,0:T(8,128)S(1)} %get-tuple-element.9) | data formatting | bytes 739328
  41.3 0.5 %copy.16 = f32[2]{0:T(128)} copy(f32[2]{0:T(128)S(1)} %get-tuple-element.16) | data formatting | bytes 16
Async XLA Ops:
  0.6 1.3 %copy-start = (bf16[608,640]{1,0:T(8,128)(2,1)S(1)}, bf16[608,640]{1,0:T(8,128)(2,1)}, u32[]{:S(2)}) copy-start(bf16[608,640]{1,0:T(8,128)(2,1)} %constant.11.clone.ol_hbm) | copy-start | bytes 2334724
  0.6 1.2 %copy-start.7 = (f32[2]{0:T(128)S(1)}, f32[2]{0:T(128)}, u32[]{:S(2)}) copy-start(f32[2]{0:T(128)} %mass_ref.1) | copy-start | bytes 28
  0.7 1.2 %copy-start.6 = (f32[2]{0:T(128)S(1)}, f32[2]{0:T(128)}, u32[]{:S(2)}) copy-start(f32[2]{0:T(128)} %strength_ref.1) | copy-start | bytes 28
  0.7 1.2 %copy-start.5 = (s32[2]{0:T(128)S(1)}, s32[2]{0:T(128)}, u32[]{:S(2)}) copy-start(s32[2]{0:T(128)} %order_ref.1) | copy-start | bytes 28
  0.7 1.2 %copy-start.4 = (s32[1216]{0:T(1024)S(1)}, s32[1216]{0:T(1024)}, u32[]{:S(2)}) copy-start(s32[1216]{0:T(1024)} %limit_ref.1) | copy-start | bytes 14596
  1.9 1.1 %copy-start.1 = (bf16[608,640]{1,0:T(8,128)(2,1)S(1)}, bf16[608,640]{1,0:T(8,128)(2,1)}, u32[]{:S(2)}) copy-start(bf16[608,640]{1,0:T(8,128)(2,1)} %constant.10.clone.oh_hbm) | copy-start | bytes 2334724
  3.0 1.1 %copy-start.2 = (bf16[608,640]{1,0:T(8,128)(2,1)S(1)}, bf16[608,640]{1,0:T(8,128)(2,1)}, u32[]{:S(2)}) copy-start(bf16[608,640]{1,0:T(8,128)(2,1)} %constant.9.clone.el_hbm) | copy-start | bytes 2334724
  4.2 1.1 %copy-start.3 = (bf16[608,640]{1,0:T(8,128)(2,1)S(1)}, bf16[608,640]{1,0:T(8,128)(2,1)}, u32[]{:S(2)}) copy-start(bf16[608,640]{1,0:T(8,128)(2,1)} %constant.8.clone.eh_hbm) | copy-start | bytes 2334724
where the time goes:
time: 43.9 us; the launch traced here: 43.6 us
  Pallas kernels  35 us (80%)
  local copies, waits for them, and re-layouts  6.06 us (14%)
  between operations  2.51 us (6%)
    pallas_call x1, Pallas kernels, local(): pl.pallas_call(kernel, out_shape=(jax.ShapeDtypeStruct(grid_field.shape,...  35 us
    unnamed x19, local copies, waits for them, and re-layouts  6.06 us

commit v1 on v0

v1 whole, which is shorter than its diff:
```python
import math

import jax
import jax.numpy as jnp
import numpy as np
from jax import lax
from jax.experimental import pallas as pl
from jax.experimental.pallas import tpu as pltpu
from jax.sharding import PartitionSpec as P

MESH = pl.DeviceIdType.MESH
f32, bf16 = jnp.float32, jnp.bfloat16

LENGTH = 1216
HALF = LENGTH // 2
PAD = 640
ROWS = 38
PITCH = 40
GROUP = 76
PEERS = 32


def basis(parity):
    index = np.arange(HALF, dtype=np.int64)
    if parity == 0:
        phase = (index[:, None] * index[None, :]) % HALF
        angle = phase.astype(np.float64) * (2.0 * math.pi / HALF)
    else:
        phase = ((2 * index[:, None] + 1) * (2 * index[None, :] + 1)) % (4 * HALF)
        angle = phase.astype(np.float64) * (2.0 * math.pi / (4 * HALF))
    table = np.zeros((HALF, PAD), np.float32)
    table[:, :HALF] = np.cos(angle) + np.sin(angle)
    high = table.astype(bf16)
    low = (table - high.astype(np.float32)).astype(bf16)
    return np.concatenate([high, low], axis=1)


def dot(a, b):
    return jnp.dot(a, b, preferred_element_type=f32)


def split(values):
    high = values.astype(bf16)
    return high, (values - high.astype(f32)).astype(bf16)


def lanes(shape):
    return lax.broadcasted_iota(jnp.int32, shape, len(shape) - 1)


def pack(block, extra=None):
    third, fourth = block[24:32], block[32:40]
    lane = lanes((8, 128))
    tail = [
        pltpu.roll(third, 76, 1),
        pltpu.roll(fourth, 76, 1),
        jnp.where(lane < 100, pltpu.roll(third, 24, 1), pltpu.roll(fourth, 48, 1)),
    ]
    if extra is not None:
        tail[2] = jnp.where(lane < 124, tail[2], extra)
    return [jnp.where(lane < GROUP, block[8 * i : 8 * i + 8], tail[i]) for i in range(3)]


def unpack(first, second, third):
    lane = lanes((8, 128))
    return [
        first,
        second,
        third,
        jnp.where(lane < 52, pltpu.roll(first, 52, 1), pltpu.roll(third, 104, 1)),
        jnp.where(lane < 52, pltpu.roll(second, 52, 1), pltpu.roll(third, 80, 1)),
    ]


def chip_of(parity, group):
    return (group // 2) * 4 + (group % 2) * 2 + parity


def kernel(
    x_ref, limit_ref, order_ref, strength_ref, mass_ref, even_hbm, odd_hbm,
    out_ref, value_ref,
    limit, order_all, strength_all, mass, xin, tables, xs, ybuf, wbuf, gbuf, damp,
    send1, recv1, send2, recv2, esend, erecv, lsend, lrecv, tsend, trecv,
    x_sem, table_sem, small_sem, go, s1, r1, s2, r2, es, er, ls, lr, ts, tr,
):
    lev = lax.axis_index("lev")
    me = lax.axis_index("wav")
    core = me % 2
    chip_x = (me // 2) % 4
    chip_y = me // 8
    parity_me = chip_x % 2
    group_me = chip_y * 2 + chip_x // 2

    arrive = [pltpu.make_async_copy(x_ref.at[:, s], xin.at[s], x_sem.at[s]) for s in range(2)]
    loads = [
        pltpu.make_async_copy(source, tables.at[i, pl.ds(0, HALF)], table_sem.at[i])
        for i, source in enumerate((even_hbm, odd_hbm))
    ]
    small = [
        pltpu.make_async_copy(source, target, small_sem.at[i])
        for i, (source, target) in enumerate(
            ((limit_ref, limit), (order_ref, order_all), (strength_ref, strength_all), (mass_ref, mass))
        )
    ]
    for copy in arrive + loads + small:
        copy.start()

    barrier = pltpu.get_barrier_semaphore()

    def greet(k, carry):
        chip = (me // 2 + k) % 16
        pl.semaphore_signal(barrier, inc=1, device_id=(lev, chip * 2 + 1), device_id_type=MESH)
        return carry

    def greet_lev(k, carry):
        pl.semaphore_signal(barrier, inc=1, device_id=((lev + k) % 8, me), device_id_type=MESH)
        return carry

    lax.fori_loop(1, 16, greet, 0)

    @pl.when(core == 0)
    def _():
        greet(0, 0)
        lax.fori_loop(1, 8, greet_lev, 0)

    def enter():
        @pl.when(core == 1)
        def _():
            pl.semaphore_wait(barrier, PEERS - 1)
            pl.semaphore_signal(go, inc=1, device_id=(lev, me - 1), device_id_type=MESH)

        @pl.when(core == 0)
        def _():
            pl.semaphore_wait(go, 1)

    def exchange(send, recv, ssem, rsem, e):
        return pltpu.make_async_remote_copy(
            src_ref=send.at[e], dst_ref=recv.at[me], send_sem=ssem.at[e], recv_sem=rsem.at[me],
            device_id=(lev, e), device_id_type=MESH,
        )

    def await_from(send, recv, ssem, rsem, e):
        pltpu.make_async_remote_copy(
            src_ref=send.at[e], dst_ref=recv.at[e], send_sem=ssem.at[e], recv_sem=rsem.at[e],
            device_id=(lev, e), device_id_type=MESH,
        ).wait_recv()

    first_copy = (send1, recv1, s1, r1)
    second_copy = (send2, recv2, s2, r2)

    def over_peers(body):
        def step(k, carry):
            body((me + k) % PEERS)
            return carry

        lax.fori_loop(1, PEERS, step, 0)

    with jax.named_scope("t1_x"):
        tables[:, HALF:, :] = jnp.zeros((2, PAD - HALF, 2 * PAD), bf16)
        xs[:, 32:40, :] = jnp.zeros((2, 8, 1280), f32)
        xs[:, :, 1152:] = jnp.zeros((2, 40, 128), f32)
        for s in range(2):
            arrive[s].wait()
            xs[s, :ROWS, :LENGTH] = xin[s]
    lane640 = lanes((PITCH, PAD))
    folded = [[], []]
    for s in range(2):
        whole = xs[s]
        lower = jnp.where(lane640 < HALF, whole[:, :PAD], 0.0)
        upper = pltpu.roll(whole, 1280 - HALF, 1)[:, :PAD]
        folded[0].append(lower + upper)
        folded[1].append(lower - upper)

    def spread(parity):
        for g in range(8):
            tile, offset = divmod(GROUP * g, 128)
            lane = lanes((80, 128))
            piece = ybuf[:, 128 * tile : 128 * tile + 128]
            if offset:
                piece = pltpu.roll(piece, 128 - offset, 1)
            if offset + GROUP > 128:
                after = pltpu.roll(ybuf[:, 128 * tile + 128 : 128 * tile + 256], 128 - offset, 1)
                piece = jnp.where(lane < 128 - offset, piece, after)
            for c in range(2):
                packed = pack(piece[PITCH * c : PITCH * c + PITCH])
                e = chip_of(parity, g) * 2 + c
                for i in range(3):
                    send1[e, 8 * i : 8 * i + 8, :] = packed[i]

    def start_all(copy, peers):
        for e in peers[:-1]:
            exchange(*copy, e).start()

        @pl.when(peers[-1] != me)
        def _():
            exchange(*copy, peers[-1]).start()

    def column_peers(parity):
        return [
            ((chip_y + dy) % 4) * 8 + (parity + 2 * ((chip_x // 2 + j) % 2)) * 2 + (core + dc) % 2
            for dy in (2, 1, 3, 0) for j in (1, 0) for dc in (1, 0)
        ]

    def row_peers(parity):
        return [
            (parity + 2 * ((chip_y // 2 + j) % 2)) * 8 + ((chip_x + dx) % 4) * 2 + (core + dc) % 2
            for dx in (2, 1, 3, 0) for j in (1, 0) for dc in (1, 0)
        ]

    for parity in range(2):
        with jax.named_scope(f"t2_stage1_{parity}"):
            high, low = split(jnp.concatenate(folded[parity], axis=0))
            loads[parity].wait()
            both = dot(jnp.concatenate([high, low], axis=0), tables[parity, :, :PAD])
            ybuf[...] = both[:80] + both[80:] + dot(high, tables[parity, :, PAD:])
            spread(parity)
        if parity == 0:
            with jax.named_scope("t3_enter"):
                enter()
        with jax.named_scope(f"t4_send1_{parity}"):
            start_all(first_copy, column_peers(parity))
    recv1[me] = send1[me]

    with jax.named_scope("t5_damp"):
        for copy in small:
            copy.wait()
        order = order_all[core]
        strength = strength_all[core]

        def place(l, carry):
            value = limit[2 * (GROUP * group_me + l) + parity_me]
            return jnp.where(lanes((8, 128)) == l, value, carry)

        limits = lax.fori_loop(0, GROUP, place, jnp.full((8, 128), -1, jnp.int32))[:1]
        lane1 = lanes((1, 128))
        twice1 = 2 * (GROUP * group_me + lane1) + parity_me
        wave1 = jnp.minimum(twice1, LENGTH - twice1).astype(f32)
        index2 = lax.broadcasted_iota(jnp.int32, (PAD, 128), 0)
        for parity in range(2):
            twice2 = 2 * index2 + parity
            wave2 = jnp.minimum(twice2, LENGTH - twice2)
            first = wave2.astype(f32)
            radius = (wave1 * wave1 + first * first) / float(HALF) ** 2
            square = radius * radius
            powered = jnp.where(order >= 2, square, radius)
            powered = jnp.where(order >= 3, square * radius, powered)
            powered = jnp.where(order >= 4, square * square, powered)
            kept = (wave2 <= limits) & (lane1 < GROUP) & (index2 < HALF)
            damp[parity] = jnp.where(
                kept, (1.0 / float(LENGTH) ** 2) / (1.0 + strength * powered), 0.0
            )
        wbuf[:, HALF:, :] = jnp.zeros((2, PAD - HALF, 128), f32)
        gbuf[:, HALF:] = jnp.zeros((2, PAD - HALF, 128), f32)

    with jax.named_scope("t6_wait1"):
        over_peers(lambda e: await_from(*first_copy, e))
    with jax.named_scope("t7_stage2"):
        for d in range(16):
            near = [recv1[d, 8 * i : 8 * i + 8] for i in range(3)]
            far = [recv1[d + 16, 8 * i : 8 * i + 8] for i in range(3)]
            for parity in range(2):
                packed = [a + b if parity == 0 else a - b for a, b in zip(near, far)]
                pieces = unpack(*packed)
                for i in range(5):
                    count = 8 if i < 4 else ROWS - 32
                    start = ROWS * d + 8 * i
                    wbuf[parity, start : start + count, :] = pieces[i][:count]
        energy = jnp.zeros((8, 128), f32)
        blank = jnp.zeros((PAD, 128), bf16)

        def stacked(values):
            high, low = split(values)
            return jnp.concatenate(
                [jnp.concatenate([high, low], axis=1), jnp.concatenate([high, blank], axis=1)], axis=0
            )

        spectra = []
        for parity in range(2):
            both = dot(tables[parity], stacked(wbuf[parity]))
            damped = (both[:, :128] + both[:, 128:]) * damp[parity]
            energy = energy + jnp.sum((damped * damped).reshape(PAD // 8, 8, 128), axis=0)
            spectra.append(stacked(damped))
        partial_value = jnp.full((8, 128), jnp.sum(energy))
        esend[...] = mass[core] * partial_value

    def energy_to(e):
        return pltpu.make_async_remote_copy(
            src_ref=esend, dst_ref=erecv.at[me], send_sem=es.at[e // 2], recv_sem=er.at[me],
            device_id=(lev, e), device_id_type=MESH,
        )

    def energy_from(e):
        return pltpu.make_async_remote_copy(
            src_ref=esend, dst_ref=erecv.at[e], send_sem=es.at[0], recv_sem=er.at[e],
            device_id=(lev, e), device_id_type=MESH,
        )

    def level_to(e):
        return pltpu.make_async_remote_copy(
            src_ref=lsend, dst_ref=lrecv.at[lev], send_sem=ls.at[e], recv_sem=lr.at[lev],
            device_id=(e, me), device_id_type=MESH,
        )

    def level_from(e):
        return pltpu.make_async_remote_copy(
            src_ref=lsend, dst_ref=lrecv.at[e], send_sem=ls.at[e], recv_sem=lr.at[e],
            device_id=(e, me), device_id_type=MESH,
        )

    def total_to(e):
        return pltpu.make_async_remote_copy(
            src_ref=tsend, dst_ref=trecv, send_sem=ts, recv_sem=tr,
            device_id=(lev, e), device_id_type=MESH,
        )

    def over_heads(body, first):
        def step(k, carry):
            body(((me // 2 + k) % 16) * 2)
            return carry

        lax.fori_loop(first, 16, step, 0)

    def over_levels(body):
        def step(k, carry):
            body((lev + k) % 8)
            return carry

        lax.fori_loop(1, 8, step, 0)

    for part in range(2):
        with jax.named_scope(f"t8_stage3_{part}"):
            rows = slice(304 * part, 304 * part + 304)
            for parity in range(2):
                both = dot(tables[parity, rows], spectra[parity])
                gbuf[parity, rows] = both[:, :128] + both[:, 128:]
            for d in range(8 * part, 8 * part + 8):
                count = PITCH if d % 8 < 7 or part == 1 else ROWS
                even = gbuf[0, ROWS * d : ROWS * d + count]
                odd = gbuf[1, ROWS * d : ROWS * d + count]
                if count < PITCH:
                    even = jnp.concatenate([even, jnp.zeros((PITCH - count, 128), f32)], axis=0)
                    odd = jnp.concatenate([odd, jnp.zeros((PITCH - count, 128), f32)], axis=0)
                for e, block in ((d, even + odd), (d + 16, even - odd)):
                    packed = pack(block, partial_value)
                    for i in range(3):
                        send2[e, 8 * i : 8 * i + 8, :] = packed[i]
        if part == 0:
            with jax.named_scope("t9_esend"):
                over_heads(lambda e: energy_to(e).start(), 1)

                @pl.when(core == 1)
                def _():
                    energy_to(me - 1).start()

        with jax.named_scope(f"ta_send2_{part}"):
            start_all(second_copy, row_peers(part))
    recv2[me] = send2[me]

    with jax.named_scope("tb_energy"):
        @pl.when(core == 0)
        def _():
            erecv[me] = esend[...]
            over_peers(lambda e: energy_from(e).wait_recv())
            plane = erecv[0]
            for e in range(1, PEERS):
                plane = plane + erecv[e]
            lsend[...] = plane
            lrecv[lev] = plane
            pl.semaphore_wait(barrier, 7)
            over_levels(lambda e: level_to(e).start())

    with jax.named_scope("tc_wait2"):
        over_peers(lambda e: await_from(*second_copy, e))
    with jax.named_scope("td_stage4"):
        results = []
        for parity in range(2):
            halves = []
            for c in range(2):
                tiles = [None] * 5
                for g in range(8):
                    e = chip_of(parity, g) * 2 + c
                    pieces = unpack(*[recv2[e, 8 * i : 8 * i + 8] for i in range(3)])
                    tile, offset = divmod(GROUP * g, 128)
                    block = jnp.concatenate(pieces, axis=0)
                    if offset:
                        block = pltpu.roll(block, offset, 1)
                    lane = lanes((PITCH, 128))
                    if tiles[tile] is None:
                        tiles[tile] = block
                    else:
                        tiles[tile] = jnp.where(lane < offset, tiles[tile], block)
                    if offset + GROUP > 128:
                        tiles[tile + 1] = block
                tiles[4] = jnp.where(lanes((PITCH, 128)) < HALF - 512, tiles[4], 0.0)
                halves.append(jnp.concatenate(tiles, axis=1))
            high, low = split(jnp.concatenate(halves, axis=0))
            both = dot(jnp.concatenate([high, low], axis=0), tables[parity, :, :PAD])
            results.append(both[:80] + both[80:] + dot(high, tables[parity, :, PAD:]))
        sums = results[0] + results[1]
        differences = results[0] - results[1]
        none = jnp.zeros((80, PAD), f32)
        whole = jnp.concatenate([sums, none], axis=1) + pltpu.roll(
            jnp.concatenate([differences, none], axis=1), HALF, 1
        )
        for s in range(2):
            out_ref[s] = whole[PITCH * s : PITCH * s + ROWS, :LENGTH]
        for c in range(2):
            slab = recv2[c, 16:24]
            for e in range(2 + c, PEERS, 2):
                slab = slab + recv2[e, 16:24]
            value_ref[c] = slab

    with jax.named_scope("te_total"):
        @pl.when(core == 0)
        def _():
            over_levels(lambda e: level_from(e).wait_recv())
            total = lrecv[0]
            for e in range(1, 8):
                total = total + lrecv[e]
            tsend[...] = total * (1.0 / 16.0)
            total_to(me + 1).start()
            value_ref[2] = tsend[...]
            total_to(me + 1).wait_send()

        @pl.when(core == 1)
        def _():
            total_to(me - 1).wait_recv()
            value_ref[2] = trecv[...]

    with jax.named_scope("tf_drain"):
        over_peers(lambda e: exchange(*first_copy, e).wait_send())
        over_peers(lambda e: exchange(*second_copy, e).wait_send())
        over_heads(lambda e: energy_to(e).wait_send(), 1)

        @pl.when(core == 1)
        def _():
            energy_to(me - 1).wait_send()

        @pl.when(core == 0)
        def _():
            over_levels(lambda e: level_to(e).wait_send())


def leave_kernel(field_ref, value_ref, out_ref, energy_ref, total_ref, energies, total, sems):
    copies = [pltpu.make_async_copy(field_ref.at[s], out_ref.at[:, s], sems.at[s]) for s in range(2)]
    for copy in copies:
        copy.start()
    energies[0] = value_ref[0, 0, 124]
    energies[1] = value_ref[1, 0, 124]
    total[0] = value_ref[2, 0, 0]
    copies.append(pltpu.make_async_copy(energies, energy_ref, sems.at[2]))
    copies.append(pltpu.make_async_copy(total, total_ref, sems.at[3]))
    for copy in copies[2:]:
        copy.start()
    for copy in copies:
        copy.wait()


def local(grid_field, truncation_limit, diffusion_order, diffusion_strength, mass_weight):
    table_list = [jnp.asarray(basis(parity)) for parity in range(2)]
    vmem = pl.BlockSpec(memory_space=pltpu.VMEM)
    hbm = pl.BlockSpec(memory_space=pltpu.HBM)
    dma = pltpu.SemaphoreType.DMA
    blocks = pltpu.VMEM((PEERS, 24, 128), f32)
    word = pltpu.VMEM((8, 128), f32)
    field, values = pl.pallas_call(
        kernel,
        out_shape=(
            jax.ShapeDtypeStruct(grid_field.shape, f32),
            jax.ShapeDtypeStruct((3, 8, 128), f32),
        ),
        in_specs=[hbm] * 7,
        out_specs=(vmem, vmem),
        scratch_shapes=[
            pltpu.SMEM((LENGTH,), jnp.int32),
            pltpu.SMEM((2,), jnp.int32),
            pltpu.SMEM((2,), f32),
            pltpu.SMEM((2,), f32),
            pltpu.VMEM((2, ROWS, LENGTH), f32),
            pltpu.VMEM((2, PAD, 2 * PAD), bf16),
            pltpu.VMEM((2, PITCH, 1280), f32),
            pltpu.VMEM((80, PAD), f32),
            pltpu.VMEM((2, PAD, 128), f32),
            pltpu.VMEM((2, PAD, 128), f32),
            pltpu.VMEM((2, PAD, 128), f32),
            blocks, blocks, blocks, blocks,
            word, pltpu.VMEM((PEERS, 8, 128), f32), word, pltpu.VMEM((8, 8, 128), f32), word, word,
            dma((2,)), dma((2,)), dma((4,)), pltpu.SemaphoreType.REGULAR,
            dma((PEERS,)), dma((PEERS,)), dma((PEERS,)), dma((PEERS,)),
            dma((16,)), dma((PEERS,)), dma((8,)), dma((8,)), dma, dma,
        ],
        compiler_params=pltpu.CompilerParams(
            collective_id=0, has_side_effects=True, vmem_limit_bytes=48 * 1024 * 1024
        ),
    )(
        *[
            pltpu.with_memory_space_constraint(operand, pltpu.HBM)
            for operand in (
                jnp.transpose(grid_field, (1, 0, 2)), truncation_limit, diffusion_order,
                diffusion_strength, mass_weight, *table_list,
            )
        ]
    )
    filtered, energies, total = pl.pallas_call(
        leave_kernel,
        out_shape=(
            jax.ShapeDtypeStruct((ROWS, 2, LENGTH), f32),
            jax.ShapeDtypeStruct((2,), f32),
            jax.ShapeDtypeStruct((1,), f32),
        ),
        in_specs=[vmem, vmem],
        out_specs=(hbm, hbm, hbm),
        scratch_shapes=[pltpu.SMEM((2,), f32), pltpu.SMEM((1,), f32), dma((4,))],
        compiler_params=pltpu.CompilerParams(vmem_limit_bytes=8 * 1024 * 1024),
    )(field, values)
    return jnp.transpose(filtered, (1, 0, 2)), energies, total.reshape(())


def solution(mesh):
    placed = (P("lev", "wav", None), P(), P("lev"), P("lev"), P("lev"))
    return jax.shard_map(
        local,
        mesh=mesh,
        in_specs=placed,
        out_specs=(P("lev", "wav", None), P("lev"), P()),
        check_vma=False,
    )
```

time: 43.9 us -> 36.8 us (0.84)
  local copies, waits for them, and re-layouts: 6.06 us -> 0 us
  between operations: 2.51 us -> 0.64 us
  Pallas kernels: 35 us -> 36 us
    unnamed x19 -> x0, local copies, waits for them, and re-layouts: 6.06 us -> none
    pallas_call x0 -> x1, Pallas kernels: none -> 0.79 us  [local(): pl.pallas_call(leave_kernel, out_shape=(jax.ShapeDtypeStruct((ROWS, 2, LE...]
where the time goes in v1:
time: 36.8 us; the launch traced here: 36.7 us
  Pallas kernels  36 us (98%)
  between operations  0.64 us (2%)
    pallas_call x1, Pallas kernels, local(): pl.pallas_call(kernel, out_shape=(jax.ShapeDtypeStruct(grid_field.shape,...  35.2 us
    pallas_call x1, Pallas kernels, local(): pl.pallas_call(leave_kernel, out_shape=(jax.ShapeDtypeStruct((ROWS, 2, LE...  0.79 us

profile of v1, /device:TPU:1, one launch (start us, length us, event | category | flops | bytes accessed | tf_op | source)
XLA Modules:
  0.0 36.7 jit_solution(10614768975984361132)
XLA Ops:
  0.6 35.2 %shard_map.94 = (f32[2,38,1216]{2,1,0:T(8,128)S(1)}, f32[3,8,128]{2,1,0:T(8,128)S(1)}) custom-call(f32[38,2,1216]{2,1,0:T(2,128)} %bitcast.3, s32[1216]{0:T(1024)} %limit_ref.1, s32[2]{0:T(128)} %order_ref.1, f32[2]{0:T(128)} %strength_ref.1, f32[2]{0:T(128)} %mass_ref.1, bf16[608,1280]{1,0:T(8,128)(2,1)} %constant.4.clone.even_hbm, ...), custom_call_target="tpu_custom_call" | custom-call | tf_op jit(solution)/shard_map/pallas_call | solution.py:466
  35.9 0.8 %shard_map.95 = (f32[38,2,1216]{2,1,0:T(2,128)}, f32[2]{0:T(128)}, f32[1]{0:T(128)}) custom-call(f32[2,38,1216]{2,1,0:T(8,128)S(1)} %get-tuple-element.8.field_ref, f32[3,8,128]{2,1,0:T(8,128)S(1)} %get-tuple-element.9.value_ref), custom_call_target="tpu_custom_call" | custom-call | tf_op jit(solution)/shard_map/pallas_call | solution.py:504
